TPU v7x, 32 devices: a whole 2x2x4 slice. The times are simulated.
32 devices in a mesh: dp: 4 (over x, core), vocab: 8 (over z, y).
Axes of the slice: x: 2, y: 2, z: 4, core: 2. Of those that a mesh axis runs over, the one named last changes fastest.
Arguments:
- hidden: bfloat16 [512, 8192], P('dp'), may hold values from -600 to 600
- out_weight: bfloat16 [8192, 98304], P('dp', 'vocab'), may hold values from -0.5 to 0.5
- targets: int32 [512], P('dp'), may hold values from 0 to 98303
- segment: int32 [512], P('dp'), may hold values from 0 to 15, never falling along the last dimension, each value on 1 to 64 neighbouring positions
- loss_mask: int32 [512], P('dp'), may hold values 0 or 1
- outside_count: int32 [16], replicated, may hold values from 0 to 3
Outputs:
- token_loss: float32 [512], P('dp')
- sample_loss: float32 [16], replicated
All inputs are finite; a program needn't handle non-finite values. No bound on the sum of `loss_mask` on one device may be relied on, other than what follows from the above.
Results may differ from a plain program's by a relative error of at most 0.0003.
Values may be sent and summed in bfloat16 or wider, within the bound.
A program may use at most 128 MiB of HBM per device.

v0:
```python
import functools

import jax
import jax.numpy as jnp
from jax import lax
from jax.experimental import pallas as pl
from jax.experimental.pallas import tpu as pltpu
from jax.sharding import PartitionSpec as P

LANES = 128
TOP = 32767.0
TINY = 1e-30


def largest_tile(columns, most):
    tile = most
    while columns % tile:
        tile //= 2
    return tile


def kernel(dims, hidden, weight, targets, segment, mask, outside, loss_out, sample_out,
           hx, wbuf, ybuf, prt, qs, qr, ss, sr, scale_buf, tg, tcol, m_buf, s_buf, p_buf,
           stat, statr, samp, wsem, local_sem, hsem, csem_s, csem_r, fsem_s, fsem_r, tsem,
           ysem, prsem, qssem, qrsem, sssem, srsem, stsem, strsem, spsem, sprsem):
    dp, nv, rows, depth, tiles, tile, chunks = dims
    chips = dp // 2
    me, v = lax.axis_index("dp"), lax.axis_index("vocab")
    x, c = me // 2, me % 2
    partner = 2 * x + (1 - c)
    owner = 2 * lax.rem(x + 1, chips) + c
    source = 2 * lax.rem(x + chips - 1, chips) + c
    share = rows // chunks

    def remote(src, dst, send, recv, d, w):
        return pltpu.make_async_remote_copy(
            src_ref=src, dst_ref=dst, send_sem=send, recv_sem=recv,
            device_id=(d, w), device_id_type=pl.DeviceIdType.MESH)

    def wcopy(t, slot):
        return pltpu.make_async_copy(
            weight.at[:, pl.ds(pl.multiple_of(t * tile, tile), tile)], wbuf.at[slot], wsem.at[slot])

    def features(d):
        return pl.ds(pl.multiple_of(d * depth, depth), depth)

    def token_rows(d):
        return pl.ds(pl.multiple_of(d * rows, rows), rows)

    def chunk_rows(d, j):
        return pl.ds(pl.multiple_of(d * rows + j * share, share), share)

    wcopy(0, 0).start()
    own = pltpu.make_async_copy(hidden.at[:, features(me)], hx.at[token_rows(me)], local_sem)
    own.start()

    barrier = pltpu.get_barrier_semaphore()

    def greet(d, w):
        pl.semaphore_signal(barrier, inc=1, device_id=(d, w), device_id_type=pl.DeviceIdType.MESH)

    for o in range(1, dp):
        greet(lax.rem(me + o, dp), v)

    columns_met = [0, 1] if chips == 2 else [0, 1, chips - 1]

    def greet_vocab(o, carry):
        w = lax.rem(v + o, nv)
        for step in columns_met:
            greet(2 * lax.rem(x + step, chips) + c, w)
        return carry

    lax.fori_loop(1, nv, greet_vocab, 0)
    pl.semaphore_wait(barrier, dp - 1 + (nv - 1) * len(columns_met))

    to_partner = remote(hidden.at[:, features(partner)], hx.at[token_rows(me)],
                        hsem.at[0], hsem.at[1], partner, v)
    to_partner.start()
    targets_copy = remote(targets, tg, tsem.at[0], tsem.at[1], source, v)

    def crossing(step, e):
        d = 2 * lax.rem(x + step, chips) + e
        src = hidden.at[pl.ds(pl.multiple_of(v * share, share), share), features(d)]
        i = 2 * (step - 1) + e
        r = 2 * (chips - step - 1) + c
        return d, src, i, r

    def cross_start():
        for step in range(1, chips):
            for e in range(2):
                d, src, i, r = crossing(step, e)
                remote(src, hx.at[chunk_rows(me, v)], csem_s.at[i], csem_r.at[r], d, v).start()

    if chunks < nv:
        pl.when(v < chunks)(cross_start)
    else:
        cross_start()
    targets_copy.start()

    def spread_each(step, e, do):
        d = 2 * lax.rem(x + step, chips) + e
        i = 2 * (step - 1) + e

        def one(o, carry):
            w = lax.rem(v + o, nv)
            block = hx.at[chunk_rows(d, v)]
            copy = remote(block, block, fsem_s.at[i, o - 1], fsem_r.at[i, v], me, w)
            do(copy)
            return carry

        lax.fori_loop(1, nv, one, 0)

    def spread():
        for step in range(1, chips):
            for e in range(2):
                d = 2 * lax.rem(x + step, chips) + e
                i = 2 * (step - 1) + e
                block = hx.at[chunk_rows(d, v)]
                remote(block, block, csem_s.at[i], csem_r.at[i], d, v).wait_recv()
                spread_each(step, e, lambda copy: copy.start())

    def spread_wait(step):
        for e in range(2):
            d = 2 * lax.rem(x + step, chips) + e
            i = 2 * (step - 1) + e

            def one(j, carry):
                @pl.when(j != v)
                def _():
                    block = hx.at[chunk_rows(d, j)]
                    remote(block, block, fsem_s.at[i, 0], fsem_r.at[i, j], me, lax.rem(v + 1, nv)).wait_recv()
                return carry

            lax.fori_loop(0, chunks, one, 0)

    def dot_tile(group, slot, yslot):
        width = min(tile, 512)
        lhs_rows = pl.ds(pl.multiple_of(group * 2 * rows, 2 * rows), 2 * rows)

        def piece(j, carry):
            cols = pl.ds(pl.multiple_of(j * width, width), width)
            ybuf[yslot, :, cols] = jnp.dot(hx[lhs_rows, :], wbuf[slot, :, cols],
                                           preferred_element_type=jnp.float32)
            return carry

        lax.fori_loop(0, tile // width, piece, 0)

    def ycopy(s, t, yslot):
        half = pl.ds(pl.multiple_of((1 - c) * rows, rows), rows)
        return remote(ybuf.at[yslot, half], prt.at[s, t], ysem.at[yslot], prsem.at[s, t], partner, v)

    def qcopy(s, t):
        d = 2 * lax.rem(x + chips - s - 1 + chips, chips) + c
        return (remote(qs.at[s, t], qr.at[s, t], qssem.at[s, t], qrsem.at[s, t], d, v),
                remote(ss.at[s, t], sr.at[s, t], sssem.at[s, t], srsem.at[s, t], d, v))

    band = min(rows, 32)

    def total(s, t, yslot, b):
        mine = pl.ds(pl.multiple_of(c * rows + b * band, band), band)
        theirs = pl.ds(b * band, band)
        return ybuf[yslot, mine, :] + prt[s, t, theirs, :]

    def send_sums(s, t, yslot):
        ycopy(s, t, yslot).wait_recv()
        for b in range(rows // band):
            value = total(s, t, yslot, b)
            top = jnp.maximum(jnp.max(jnp.abs(value), axis=1, keepdims=True), TINY)
            code = jnp.round(value * (TOP / top)).astype(jnp.int32)
            qs[s, t, b * band:(b + 1) * band, :] = code.astype(jnp.int16)
            scale_buf[b * band:(b + 1) * band, :] = jnp.broadcast_to(top * (1.0 / TOP), (band, LANES))
        ss[s, t] = jnp.transpose(scale_buf[0:rows, :])[0:8, :]
        for copy in qcopy(s, t):
            copy.start()

    def finish(s, t, yslot):
        ycopy(s, t, yslot).wait_recv()
        for a in range(chips - 1):
            for copy in qcopy(a, t):
                copy.wait_recv()
            scale_buf[a * rows:(a + 1) * rows, :] = jnp.transpose(
                jnp.broadcast_to(sr[a, t, 0:1, :], (LANES, rows)))
        base = v * (tiles * tile) + t * tile
        lane = lax.broadcasted_iota(jnp.int32, (band, LANES), 1)
        for b in range(rows // band):
            here = slice(b * band, (b + 1) * band)
            value = total(s, t, yslot, b)
            parts = []
            for k in range(tile // LANES):
                part = value[:, k * LANES:(k + 1) * LANES]
                for a in range(chips - 1):
                    code = qr[a, t, here, k * LANES:(k + 1) * LANES].astype(jnp.int32)
                    part = part + code.astype(jnp.float32) * scale_buf[a * rows + b * band:a * rows + (b + 1) * band, :]
                parts.append(part)
            old = m_buf[here, :]
            new = functools.reduce(jnp.maximum, parts, old)
            acc = s_buf[here, :] * jnp.exp(old - new)
            picked = p_buf[here, :]
            wanted = tcol[here, :] - base
            for k, part in enumerate(parts):
                acc = acc + jnp.exp(part - new)
                picked = picked + jnp.where(lane + k * LANES == wanted, part, 0.0)
            m_buf[here, :] = new
            s_buf[here, :] = acc
            p_buf[here, :] = picked

    own.wait()
    to_partner.wait_recv()
    m_buf[...] = jnp.full(m_buf.shape, -jnp.inf, jnp.float32)
    s_buf[...] = jnp.zeros(s_buf.shape, jnp.float32)
    p_buf[...] = jnp.zeros(p_buf.shape, jnp.float32)

    for s in range(chips):
        group = lax.rem(x + chips - s, chips)
        last = s == chips - 1
        if s > 0:
            spread_wait(chips - s)
        if last:
            targets_copy.wait_recv()
            tcol[...] = jnp.transpose(jnp.broadcast_to(tg[0:1, :], (LANES, rows)))
        handle = finish if last else send_sums

        def step(t, carry, s=s, group=group, last=last, handle=handle):
            i = s * tiles + t
            slot = lax.rem(i, 2)
            wcopy(t, slot).wait()

            @pl.when(i + 1 < chips * tiles)
            def _():
                wcopy(lax.rem(t + 1, tiles), 1 - slot).start()

            @pl.when(i >= 2)
            def _():
                ycopy(s, t, slot).wait_send()

            dot_tile(group, slot, slot)
            ycopy(s, t, slot).start()

            @pl.when(t >= 1)
            def _():
                handle(s, t - 1, 1 - slot)

            if s == 0:
                @pl.when(t == min(1, tiles - 1))
                def _():
                    if chunks < nv:
                        pl.when(v < chunks)(spread)
                    else:
                        spread()
            return carry

        lax.fori_loop(0, tiles, step, 0)
        handle(s, tiles - 1, (s * tiles + tiles - 1) % 2)

    lane = lax.broadcasted_iota(jnp.int32, (rows, LANES), 1)
    peak = jnp.max(m_buf[...], axis=1, keepdims=True)
    mass = jnp.sum(s_buf[...] * jnp.exp(m_buf[...] - peak), axis=1, keepdims=True)
    hit = jnp.sum(p_buf[...], axis=1, keepdims=True)
    table = jnp.where(lane == 0, peak, jnp.where(lane == 1, mass, hit))
    stat[...] = jnp.transpose(table)[0:8, :]

    def stat_copy(w):
        return remote(stat, statr.at[v], stsem.at[w], strsem.at[v], owner, w)

    def stat_start(o, carry):
        stat_copy(lax.rem(v + o, nv)).start()
        return carry

    lax.fori_loop(0, nv, stat_start, 0)

    def stat_wait(w, carry):
        remote(stat, statr.at[w], stsem.at[w], strsem.at[w], owner, w).wait_recv()
        return carry

    lax.fori_loop(0, nv, stat_wait, 0)
    peak = statr[0, 0:1, :]
    for w in range(1, nv):
        peak = jnp.maximum(peak, statr[w, 0:1, :])
    mass = jnp.zeros_like(peak)
    hit = jnp.zeros_like(peak)
    for w in range(nv):
        mass = mass + statr[w, 1:2, :] * jnp.exp(statr[w, 0:1, :] - peak)
        hit = hit + statr[w, 2:3, :]
    loss = peak + jnp.log(mass) - hit
    loss_out[...] = loss

    samples = outside.shape[0]
    weights = mask[...].astype(jnp.float32)
    member = lax.broadcasted_iota(jnp.int32, (samples, rows), 0) == segment[...]
    sums = jnp.sum(jnp.where(member, loss * weights, 0.0), axis=1, keepdims=True)
    count = jnp.sum(jnp.where(member, weights, 0.0), axis=1, keepdims=True)
    wide = lax.broadcasted_iota(jnp.int32, (samples, LANES), 1)
    samp[me] = jnp.where(wide < LANES // 2, sums, count)

    def samp_copy(o, d):
        return remote(samp.at[d], samp.at[d], spsem.at[o - 1], sprsem.at[d], lax.rem(me + o, dp), v)

    for o in range(1, dp):
        samp_copy(o, me).start()
    for o in range(1, dp):
        samp_copy(o, lax.rem(me + o, dp)).wait_recv()
    both = samp[0]
    for d in range(1, dp):
        both = both + samp[d]
    sums = both[:, 0:1]
    count = both[:, LANES - 1:LANES]
    denom = jnp.maximum(count + outside[...].astype(jnp.float32), 1.0)
    sample_out[...] = sums / denom

    to_partner.wait_send()
    targets_copy.wait_send()

    def leave():
        for step in range(1, chips):
            for e in range(2):
                d, src, i, r = crossing(step, e)
                remote(src, hx.at[chunk_rows(me, v)], csem_s.at[i], csem_r.at[r], d, v).wait_send()
                spread_each(step, e, lambda copy: copy.wait_send())

    if chunks < nv:
        pl.when(v < chunks)(leave)
    else:
        leave()
    for k in range(min(2, chips * tiles)):
        ycopy(0, 0, k).wait_send()

    def sums_left(t, carry):
        for s in range(chips - 1):
            for copy in qcopy(s, t):
                copy.wait_send()
        return carry

    lax.fori_loop(0, tiles, sums_left, 0)

    def stat_left(w, carry):
        stat_copy(w).wait_send()
        return carry

    lax.fori_loop(0, nv, stat_left, 0)
    for o in range(1, dp):
        samp_copy(o, me).wait_send()


def solution(mesh):
    dp, nv = mesh.shape["dp"], mesh.shape["vocab"]

    def body(hidden, out_weight, targets, segment, loss_mask, outside_count):
        rows = hidden.shape[0]
        depth, columns = out_weight.shape
        samples = outside_count.shape[0]
        chips = dp // 2
        tile = largest_tile(columns, 1024)
        tiles = columns // tile
        chunks = min(nv, rows // 16)
        dims = (dp, nv, rows, depth, tiles, tile, chunks)
        sem = pltpu.SemaphoreType.DMA
        far = 2 * (chips - 1)
        vm = pl.BlockSpec(memory_space=pltpu.VMEM)
        hbm = pl.BlockSpec(memory_space=pl.ANY)
        loss, sample = pl.pallas_call(
            functools.partial(kernel, dims),
            out_shape=(jax.ShapeDtypeStruct((1, rows), jnp.float32),
                       jax.ShapeDtypeStruct((samples, LANES), jnp.float32)),
            in_specs=[hbm, hbm, vm, vm, vm, vm],
            out_specs=(vm, vm),
            scratch_shapes=[
                pltpu.VMEM((dp * rows, depth), jnp.bfloat16),
                pltpu.VMEM((2, depth, tile), jnp.bfloat16),
                pltpu.VMEM((2, 2 * rows, tile), jnp.float32),
                pltpu.VMEM((chips, tiles, rows, tile), jnp.float32),
                pltpu.VMEM((chips - 1, tiles, rows, tile), jnp.int16),
                pltpu.VMEM((chips - 1, tiles, rows, tile), jnp.int16),
                pltpu.VMEM((chips - 1, tiles, 8, rows), jnp.float32),
                pltpu.VMEM((chips - 1, tiles, 8, rows), jnp.float32),
                pltpu.VMEM(((chips - 1) * rows, LANES), jnp.float32),
                pltpu.VMEM((8, rows), jnp.int32),
                pltpu.VMEM((rows, LANES), jnp.int32),
                pltpu.VMEM((rows, LANES), jnp.float32),
                pltpu.VMEM((rows, LANES), jnp.float32),
                pltpu.VMEM((rows, LANES), jnp.float32),
                pltpu.VMEM((8, rows), jnp.float32),
                pltpu.VMEM((nv, 8, rows), jnp.float32),
                pltpu.VMEM((dp, samples, LANES), jnp.float32),
                sem((2,)), sem, sem((2,)), sem((far,)), sem((far,)),
                sem((far, nv - 1)), sem((far, chunks)), sem((2,)),
                sem((2,)), sem((chips, tiles)),
                sem((chips - 1, tiles)), sem((chips - 1, tiles)),
                sem((chips - 1, tiles)), sem((chips - 1, tiles)),
                sem((nv,)), sem((nv,)), sem((dp - 1,)), sem((dp,)),
            ],
            compiler_params=pltpu.CompilerParams(
                collective_id=0, has_side_effects=True, vmem_limit_bytes=60 * 1024 * 1024),
        )(hidden, out_weight,
          jnp.broadcast_to(targets[None, :], (8, rows)),
          segment[None, :], loss_mask[None, :],
          jnp.broadcast_to(outside_count[:, None], (samples, LANES)))
        return loss[0], sample[:, 0]

    return jax.shard_map(
        body,
        mesh=mesh,
        in_specs=(P("dp", None), P("dp", "vocab"), P("dp"), P("dp"), P("dp"), P()),
        out_specs=(P("dp"), P()),
        check_vma=False,
    )
```

profile of v0, /device:TPU:0, one launch (start us, length us, event | category | flops | bytes accessed | tf_op | source)
XLA Modules:
  0.0 97.2 jit_solution(14418061767474887395)
XLA Ops:
  0.6 1.2 %broadcast_in_dim.8.targets = s32[8,128]{1,0:T(8,128)} broadcast(s32[128]{0:T(128)} %param.8), dimensions={1} | broadcast | bytes 4608 | tf_op jit(solution)/shard_map/broadcast_in_dim | solution.py:394
  1.9 1.3 %broadcast_in_dim.21.outside = s32[16,128]{1,0:T(8,128)} broadcast(s32[16]{0:T(128)} %param.11), dimensions={0} | broadcast | bytes 8256 | tf_op jit(solution)/shard_map/broadcast_in_dim | solution.py:396
  3.2 91.5 %shard_map.77 = (f32[1,128]{1,0:T(1,128)}, f32[16,128]{1,0:T(8,128)}) custom-call(bf16[128,8192]{1,0:T(8,128)(2,1)} %hidden.1, bf16[2048,12288]{1,0:T(8,128)(2,1)} %weight.1, s32[8,128]{1,0:T(8,128)} %broadcast_in_dim.8.targets, s32[1,128]{1,0:T(1,128)} %bitcast.3, s32[1,128]{1,0:T(1,128)} %bitcast.4, s32[16,128]{1,0:T(8,128)} %broadcast_in_dim.21.outside), custom_call_target="tpu_custom_call" | custom-call | tf_op jit(solution)/shard_map/pallas_call | solution.py:360
  94.7 1.3 %slice_reduce_fusion = f32[16]{0:T(128)} fusion(f32[16,128]{1,0:T(8,128)} %get-tuple-element.5), kind=kLoop, calls=%fused_computation | loop fusion | bytes 128 | tf_op jit(solution)/shard_map/slice | solution.py:397
  96.1 1.2 %copy.9 = f32[128]{0:T(128)} copy(f32[128]{0:T(128)} %bitcast.5) | data formatting | bytes 1024
where the time goes:
time: 98.1 us; the launch traced here: 97.2 us
  Pallas kernels  91.5 us (93%)
  local copies, waits for them, and re-layouts  5.06 us (5%)
    pallas_call x1, Pallas kernels, body(): pl.pallas_call(functools.partial(kernel, dims), out_shape=(jax.ShapeDtype...  91.5 us

commit v1 on v0

v1 whole, which is shorter than its diff:
```python
import functools

import jax
import jax.numpy as jnp
from jax import lax
from jax.experimental import pallas as pl
from jax.experimental.pallas import tpu as pltpu
from jax.sharding import PartitionSpec as P

LANES = 128
TOP = 32767.0
TINY = 1e-30
RING = 4
WSLOTS = 4
WIDTH = 512


def largest_tile(columns, most):
    tile = most
    while columns % tile:
        tile //= 2
    return tile


def kernel(dims, hidden, weight, targets, segment, mask, outside, out,
           hx, hp, wbuf, ybuf, prt, qs, qr, ss, sr, scale_buf, tg, tcol, m_buf, s_buf, p_buf,
           info, outv, denom, stat, statr, wsem, lsem, hsem, csem_s, csem_r, fsem_s, fsem_r,
           tsem, isem, ysem, prsem, qssem, qrsem, sssem, srsem, stsem, dsem):
    dp, nv, rows, depth, tiles, tile, chunks, rounds = dims
    chips = dp // 2
    me, v = lax.axis_index("dp"), lax.axis_index("vocab")
    x, c = me // 2, me % 2
    partner = 2 * x + (1 - c)
    owner = 2 * lax.rem(x + 1, chips) + c
    source = 2 * lax.rem(x + chips - 1, chips) + c
    share = rows // chunks
    total_steps = chips * tiles

    def remote(src, dst, send, recv, d, w):
        return pltpu.make_async_remote_copy(
            src_ref=src, dst_ref=dst, send_sem=send, recv_sem=recv,
            device_id=(d, w), device_id_type=pl.DeviceIdType.MESH)

    def wcopy(t, slot):
        return pltpu.make_async_copy(
            weight.at[:, pl.ds(pl.multiple_of(t * tile, tile), tile)], wbuf.at[slot], wsem.at[slot])

    def features(d):
        return pl.ds(pl.multiple_of(d * depth, depth), depth)

    def token_rows(d):
        return pl.ds(pl.multiple_of(d * rows, rows), rows)

    def chunk_rows(d, j):
        return pl.ds(pl.multiple_of(d * rows + j * share, share), share)

    barrier = pltpu.get_barrier_semaphore()

    def signal(sem, d, w):
        pl.semaphore_signal(sem, inc=1, device_id=(d, w), device_id_type=pl.DeviceIdType.MESH)

    for o in range(1, dp):
        signal(barrier, lax.rem(me + o, dp), v)
    pl.when(v >= 1)(lambda: signal(barrier, me, v - 1))
    pl.when(v < nv - 1)(lambda: signal(barrier, me, v + 1))

    to_stage = pltpu.make_async_copy(hidden.at[:, features(partner)], hp, lsem.at[0])
    to_stage.start()
    own = pltpu.make_async_copy(hidden.at[:, features(me)], hx.at[token_rows(me)], lsem.at[1])
    own.start()
    for k in range(min(WSLOTS - 1, total_steps)):
        wcopy(k % tiles, k).start()

    def sides(reach):
        return jnp.where(v >= reach, 1, 0) + jnp.where(v < nv - reach, 1, 0)

    pl.semaphore_wait(barrier, dp - 1 + sides(1))

    def tell(k):
        reach = 1 << k
        pl.when(v >= reach)(lambda: signal(dsem.at[k], me, v - reach))
        pl.when(v < nv - reach)(lambda: signal(dsem.at[k], me, v + reach))

    def hear(k):
        pl.semaphore_wait(dsem.at[k], sides(1 << k))

    to_partner = remote(hp, hx.at[token_rows(me)], hsem.at[0], hsem.at[1], partner, v)
    targets_copy = remote(targets, tg, tsem.at[0], tsem.at[1], source, v)

    def crossing(step, e):
        d = 2 * lax.rem(x + step, chips) + e
        src = hidden.at[pl.ds(pl.multiple_of(v * share, share), share), features(d)]
        i = 2 * (step - 1) + e
        r = 2 * (chips - step - 1) + c
        return d, src, i, r

    def cross_start():
        for step in range(1, chips):
            for e in range(2):
                d, src, i, r = crossing(step, e)
                remote(src, hx.at[chunk_rows(me, v)], csem_s.at[i], csem_r.at[r], d, v).start()

    def if_sender(fn):
        if chunks < nv:
            pl.when(v < chunks)(fn)
        else:
            fn()

    if_sender(cross_start)
    if rounds:
        tell(0)
    to_stage.wait()
    to_partner.start()

    local_info = [pltpu.make_async_copy(ref, info.at[me, k], lsem.at[2])
                  for k, ref in enumerate((segment, mask))]
    local_out = pltpu.make_async_copy(outside, outv, lsem.at[3])

    def info_copy(o, k, ref):
        return remote(ref, info.at[me, k], isem.at[0], isem.at[1], lax.rem(me + o, dp), v)

    def start_small():
        targets_copy.start()
        for o in range(1, dp):
            for k, ref in enumerate((segment, mask)):
                info_copy(o, k, ref).start()
        for copy in local_info:
            copy.start()
        local_out.start()

    def spread():
        for step in range(1, chips):
            for e in range(2):
                d = 2 * lax.rem(x + step, chips) + e
                i = 2 * (step - 1) + e
                block = hx.at[chunk_rows(d, v)]
                remote(block, block, csem_s.at[i], csem_r.at[i], d, v).wait_recv()

                def one(o, carry, block=block, step=step, i=i):
                    w = lax.rem(v + o, nv)
                    remote(block, block, fsem_s.at[i], fsem_r.at[step - 1], me, w).start()
                    return carry

                lax.fori_loop(1, nv, one, 0)

    def blocks_wait(count, sem_s, sem_r, send):
        block = hx.at[pl.ds(0, count)]
        copy = remote(block, block, sem_s, sem_r, partner, v)
        if send:
            copy.wait_send()
        else:
            copy.wait_recv()

    def spread_wait(step):
        if chunks < nv:
            pl.when(v < chunks)(lambda: blocks_wait(
                2 * (chunks - 1) * share, fsem_s.at[0], fsem_r.at[step - 1], False))
            pl.when(v >= chunks)(lambda: blocks_wait(
                2 * chunks * share, fsem_s.at[0], fsem_r.at[step - 1], False))
        else:
            blocks_wait(2 * (chunks - 1) * share, fsem_s.at[0], fsem_r.at[step - 1], False)

    def dot_rows(start, count, at, slot, yslot):
        lhs = pl.ds(pl.multiple_of(start, count), count)
        ybuf[yslot, pl.ds(pl.multiple_of(at, count), count), :] = jnp.dot(
            hx[lhs, :], wbuf[slot], preferred_element_type=jnp.float32)

    def ycopy(i):
        half = pl.ds(pl.multiple_of((1 - c) * rows, rows), rows)
        slot, ring = lax.rem(i, 2), lax.rem(i, RING)
        return remote(ybuf.at[slot, half], prt.at[ring], ysem.at[slot], prsem.at[ring], partner, v)

    def qcopy(s, t):
        d = 2 * lax.rem(x + chips - s - 1 + chips, chips) + c
        return (remote(qs.at[s, t], qr.at[s, t], qssem, qrsem.at[s, t], d, v),
                remote(ss.at[s, t], sr.at[s, t], sssem, srsem.at[s, t], d, v))

    band = min(rows, 32)

    def total(i, b):
        mine = pl.ds(pl.multiple_of(c * rows + b * band, band), band)
        theirs = pl.ds(b * band, band)
        return ybuf[lax.rem(i, 2), mine, :] + prt[lax.rem(i, RING), theirs, :]

    def send_sums(s, t):
        i = s * tiles + t
        ycopy(i).wait_recv()
        for b in range(rows // band):
            value = total(i, b)
            top = jnp.maximum(jnp.max(jnp.abs(value), axis=1, keepdims=True), TINY)
            code = jnp.round(value * (TOP / top)).astype(jnp.int32)
            qs[s, t, b * band:(b + 1) * band, :] = code.astype(jnp.int16)
            scale_buf[b * band:(b + 1) * band, :] = jnp.broadcast_to(top * (1.0 / TOP), (band, LANES))
        data, scales = qcopy(s, t)
        data.start()
        ss[s, t] = jnp.transpose(scale_buf[0:rows, :])[0:1, :]
        scales.start()

    def finish(s, t):
        i = s * tiles + t
        ycopy(i).wait_recv()
        for a in range(chips - 1):
            for copy in qcopy(a, t):
                copy.wait_recv()
            scale_buf[a * rows:(a + 1) * rows, :] = jnp.transpose(
                jnp.broadcast_to(sr[a, t], (LANES, rows)))
        base = v * (tiles * tile) + t * tile
        lane = lax.broadcasted_iota(jnp.int32, (band, LANES), 1)
        for b in range(rows // band):
            here = slice(b * band, (b + 1) * band)
            value = total(i, b)
            parts = []
            for k in range(tile // LANES):
                part = value[:, k * LANES:(k + 1) * LANES]
                for a in range(chips - 1):
                    code = qr[a, t, here, k * LANES:(k + 1) * LANES].astype(jnp.int32)
                    part = part + code.astype(jnp.float32) * scale_buf[a * rows + b * band:a * rows + (b + 1) * band, :]
                parts.append(part)
            old = m_buf[here, :]
            new = functools.reduce(jnp.maximum, parts, old)
            acc = s_buf[here, :] * jnp.exp(old - new)
            picked = p_buf[here, :]
            wanted = tcol[here, :] - base
            for k, part in enumerate(parts):
                acc = acc + jnp.exp(part - new)
                picked = picked + jnp.where(lane + k * LANES == wanted, part, 0.0)
            m_buf[here, :] = new
            s_buf[here, :] = acc
            p_buf[here, :] = picked

    m_buf[...] = jnp.full(m_buf.shape, -jnp.inf, jnp.float32)
    s_buf[...] = jnp.zeros(s_buf.shape, jnp.float32)
    p_buf[...] = jnp.zeros(p_buf.shape, jnp.float32)
    own.wait()

    events = []
    events.append((1, start_small))
    for k in range(rounds):
        def turn(k=k):
            hear(k)
            if k + 1 < rounds:
                tell(k + 1)
        events.append((2 + 2 * k, turn))
    events.append((2 + 2 * rounds, lambda: if_sender(spread)))

    samples = outside.shape[1]

    def prepare():
        targets_copy.wait_recv()
        tcol[...] = jnp.transpose(jnp.broadcast_to(tg[...], (LANES, rows)))
        most = info.at[pl.ds(0, dp - 1)]
        remote(most, most, isem.at[0], isem.at[1], partner, v).wait_recv()
        pltpu.make_async_copy(info.at[me], info.at[me], lsem.at[2]).wait()
        local_out.wait()
        count = jnp.zeros((samples, 1), jnp.float32)
        for d in range(dp):
            member = lax.broadcasted_iota(jnp.int32, (samples, rows), 0) == info[d, 0]
            weights = info[d, 1].astype(jnp.float32)
            count = count + jnp.sum(jnp.where(member, weights, 0.0), axis=1, keepdims=True)
        square = (lax.broadcasted_iota(jnp.int32, (samples, samples), 0)
                  == lax.broadcasted_iota(jnp.int32, (samples, samples), 1))
        away = jnp.sum(jnp.where(square, outv[...].astype(jnp.float32), 0.0), axis=1, keepdims=True)
        denom[...] = jnp.broadcast_to(jnp.maximum(count + away, 1.0), (samples, LANES))

    for s in range(chips):
        group = lax.rem(x + chips - s, chips)
        last = s == chips - 1
        if s > 0:
            spread_wait(chips - s)
        if last:
            prepare()
        handle = finish if last else send_sums

        def begin(i):
            slot = lax.rem(i, WSLOTS)
            wcopy(lax.rem(i, tiles), slot).wait()

            @pl.when(i + WSLOTS - 1 < total_steps)
            def _():
                wcopy(lax.rem(i + WSLOTS - 1, tiles), lax.rem(i + WSLOTS - 1, WSLOTS)).start()

            return slot

        def step(t, carry, s=s, group=group, handle=handle, begin=begin):
            i = s * tiles + t
            slot = begin(i)

            @pl.when(i >= 2)
            def _():
                ycopy(i).wait_send()

            dot_rows(group * 2 * rows, 2 * rows, 0, slot, lax.rem(i, 2))
            ycopy(i).start()

            @pl.when(t >= 1)
            def _():
                handle(s, t - 1)

            if s == 0:
                for at, event in events:
                    pl.when(t == min(at, tiles - 1))(event)
            return carry

        first = 0
        if s == 0:
            slot = begin(0)
            dot_rows(me * rows, rows, c * rows, slot, 0)
            to_partner.wait_recv()
            dot_rows(partner * rows, rows, (1 - c) * rows, slot, 0)
            ycopy(0).start()
            for at, event in events:
                if min(at, tiles - 1) == 0:
                    event()
            first = 1
        lax.fori_loop(first, tiles, step, 0)
        handle(s, tiles - 1)

    lane = lax.broadcasted_iota(jnp.int32, (rows, LANES), 1)
    peak = jnp.max(m_buf[...], axis=1, keepdims=True)
    mass = jnp.sum(s_buf[...] * jnp.exp(m_buf[...] - peak), axis=1, keepdims=True)
    hit = jnp.sum(p_buf[...], axis=1, keepdims=True)
    table = jnp.transpose(jnp.where(lane == 0, peak, jnp.where(lane == 1, mass, hit)))
    stat[0:1, :] = table[0:1, :] + jnp.log(table[1:2, :])
    stat[1:2, :] = table[2:3, :]

    def stat_copy(d, w):
        return remote(stat, statr.at[owner * nv + v], stsem.at[0], stsem.at[1], d, w)

    def stat_start(o, carry):
        w = lax.rem(v + o, nv)
        for k in range(dp):
            stat_copy(lax.rem(me + k, dp), w).start()
        return carry

    lax.fori_loop(1, nv, stat_start, 0)
    for k in range(1, dp):
        stat_copy(lax.rem(me + k, dp), v).start()
    statr[owner * nv + v] = stat[...]
    most = statr.at[pl.ds(0, dp * nv - 1)]
    remote(most, most, stsem.at[0], stsem.at[1], partner, v).wait_recv()

    mine = jnp.zeros((1, rows), jnp.float32)
    sums = jnp.zeros((samples, rows), jnp.float32)
    for d in range(dp):
        block = statr[d * nv:(d + 1) * nv]
        peak = jnp.max(block, axis=0)
        mass = jnp.sum(jnp.exp(block - peak[None]), axis=0)
        hit = jnp.sum(block, axis=0)
        loss = peak[0:1, :] + jnp.log(mass[0:1, :]) - hit[1:2, :]
        mine = jnp.where(me == d, loss, mine)
        member = lax.broadcasted_iota(jnp.int32, (samples, rows), 0) == info[d, 0]
        sums = sums + jnp.where(member, loss * info[d, 1].astype(jnp.float32), 0.0)
    ratio = jnp.sum(sums, axis=1, keepdims=True) / denom[:, 0:1]
    wide = out.shape[1] - rows
    diagonal = (lax.broadcasted_iota(jnp.int32, (samples, wide), 0)
                == lax.broadcasted_iota(jnp.int32, (samples, wide), 1))
    out[0:1, 0:rows] = mine
    out[0:1, rows:rows + wide] = jnp.sum(jnp.where(diagonal, ratio, 0.0), axis=0, keepdims=True)

    to_partner.wait_send()
    targets_copy.wait_send()
    most_info = info.at[pl.ds(0, dp - 1)]
    remote(most_info, most_info, isem.at[0], isem.at[1], partner, v).wait_send()

    def leave():
        for step in range(1, chips):
            for e in range(2):
                d, src, i, r = crossing(step, e)
                remote(src, hx.at[chunk_rows(me, v)], csem_s.at[i], csem_r.at[r], d, v).wait_send()
        for step in range(1, chips):
            for e in range(2):
                i = 2 * (step - 1) + e
                blocks_wait((nv - 1) * share, fsem_s.at[i], fsem_r.at[step - 1], True)

    if_sender(leave)
    for k in range(min(2, total_steps)):
        ycopy(k).wait_send()
    remote(qs, qr, qssem, qrsem.at[0, 0], partner, v).wait_send()
    remote(ss, sr, sssem, srsem.at[0, 0], partner, v).wait_send()
    remote(most, most, stsem.at[0], stsem.at[1], partner, v).wait_send()


def solution(mesh):
    dp, nv = mesh.shape["dp"], mesh.shape["vocab"]

    def body(hidden, out_weight, targets, segment, loss_mask, outside_count):
        rows = hidden.shape[0]
        depth, columns = out_weight.shape
        samples = outside_count.shape[0]
        chips = dp // 2
        tile = largest_tile(columns, WIDTH)
        tiles = columns // tile
        chunks = min(nv, rows // 16)
        rounds = (nv - 2).bit_length()
        dims = (dp, nv, rows, depth, tiles, tile, chunks, rounds)
        sem = pltpu.SemaphoreType.DMA
        far = 2 * (chips - 1)
        wide = -(-samples // LANES) * LANES
        vm = pl.BlockSpec(memory_space=pltpu.VMEM)
        hbm = pl.BlockSpec(memory_space=pl.ANY)
        res = pl.pallas_call(
            functools.partial(kernel, dims),
            out_shape=jax.ShapeDtypeStruct((1, rows + wide), jnp.float32),
            in_specs=[hbm] * 6,
            out_specs=vm,
            scratch_shapes=[
                pltpu.VMEM((dp * rows, depth), jnp.bfloat16),
                pltpu.VMEM((rows, depth), jnp.bfloat16),
                pltpu.VMEM((WSLOTS, depth, tile), jnp.bfloat16),
                pltpu.VMEM((2, 2 * rows, tile), jnp.float32),
                pltpu.VMEM((RING, rows, tile), jnp.float32),
                pltpu.VMEM((chips - 1, tiles, rows, tile), jnp.int16),
                pltpu.VMEM((chips - 1, tiles, rows, tile), jnp.int16),
                pltpu.VMEM((chips - 1, tiles, 1, rows), jnp.float32),
                pltpu.VMEM((chips - 1, tiles, 1, rows), jnp.float32),
                pltpu.VMEM(((chips - 1) * rows, LANES), jnp.float32),
                pltpu.VMEM((1, rows), jnp.int32),
                pltpu.VMEM((rows, LANES), jnp.int32),
                pltpu.VMEM((rows, LANES), jnp.float32),
                pltpu.VMEM((rows, LANES), jnp.float32),
                pltpu.VMEM((rows, LANES), jnp.float32),
                pltpu.VMEM((dp, 2, 1, rows), jnp.int32),
                pltpu.VMEM((1, samples), jnp.int32),
                pltpu.VMEM((samples, LANES), jnp.float32),
                pltpu.VMEM((2, rows), jnp.float32),
                pltpu.VMEM((dp * nv, 2, rows), jnp.float32),
                sem((WSLOTS,)), sem((4,)), sem((2,)), sem((far,)), sem((far,)),
                sem((far,)), sem((chips - 1,)), sem((2,)), sem((2,)),
                sem((2,)), sem((RING,)),
                sem, sem((chips - 1, tiles)), sem, sem((chips - 1, tiles)),
                sem((2,)), pltpu.SemaphoreType.REGULAR((max(rounds, 1),)),
            ],
            compiler_params=pltpu.CompilerParams(
                collective_id=0, has_side_effects=True, vmem_limit_bytes=60 * 1024 * 1024),
        )(hidden, out_weight, targets[None, :], segment[None, :], loss_mask[None, :],
          outside_count[None, :])
        return res[0, :rows], res[0, rows:rows + samples]

    return jax.shard_map(
        body,
        mesh=mesh,
        in_specs=(P("dp", None), P("dp", "vocab"), P("dp"), P("dp"), P("dp"), P()),
        out_specs=(P("dp"), P()),
        check_vma=False,
    )
```

time: 98.1 us -> 87.9 us (0.90)
  Pallas kernels: 91.5 us -> 84.8 us
  local copies, waits for them, and re-layouts: 5.06 us -> 2.28 us
    pallas_call x1, Pallas kernels: 91.5 us -> 84.8 us  [body(): pl.pallas_call(functools.partial(kernel, dims), out_shape=jax.ShapeDtypeS...]
    broadcast_in_dim x2 -> x0, local copies, waits for them, and re-layouts: 2.56 us -> none  [the longest x1 1.32 us: body(): jnp.broadcast_to(outside_count[:, None], (samples, LANES))]
    squeeze x0 -> x2, local copies, waits for them, and re-layouts: none -> 2.28 us  [body(): return (res[0, :rows], res[0, rows:rows + samples])]
    slice x1 -> x0, local copies, waits for them, and re-layouts: 1.32 us -> none  [body(): return (loss[0], sample[:, 0])]
    unnamed x1 -> x0, local copies, waits for them, and re-layouts: 1.18 us -> none
where the time goes in v1:
time: 87.9 us; the launch traced here: 87.7 us
  Pallas kernels  84.8 us (96%)
  local copies, waits for them, and re-layouts  2.28 us (3%)
    pallas_call x1, Pallas kernels, body(): pl.pallas_call(functools.partial(kernel, dims), out_shape=jax.ShapeDtypeS...  84.8 us
    squeeze x2, local copies, waits for them, and re-layouts, body(): return (res[0, :rows], res[0, rows:rows + samples])  2.28 us

profile of v1, /device:TPU:0, one launch (start us, length us, event | category | flops | bytes accessed | tf_op | source)
XLA Modules:
  0.0 87.7 jit_solution(2928564695599839345)
XLA Ops:
  0.6 84.8 %shard_map.77 = f32[1,256]{1,0:T(1,128)} custom-call(bf16[128,8192]{1,0:T(8,128)(2,1)} %hidden.1, bf16[2048,12288]{1,0:T(8,128)(2,1)} %weight.1, s32[1,128]{1,0:T(1,128)} %bitcast.8, s32[1,128]{1,0:T(1,128)} %bitcast.9, s32[1,128]{1,0:T(1,128)} %bitcast.10, s32[1,16]{1,0:T(1,128)} %bitcast.11), custom_call_target="tpu_custom_call" | custom-call | tf_op jit(solution)/shard_map/pallas_call | solution.py:401
  85.4 1.1 %slice_bitcast_fusion = f32[16]{0:T(128)} fusion(f32[1,256]{1,0:T(1,128)} %shard_map.77), kind=kLoop, calls=%fused_computation | loop fusion | bytes 128 | tf_op jit(solution)/shard_map/squeeze | solution.py:437
  86.5 1.2 %slice_bitcast_fusion.1 = f32[128]{0:T(128)} fusion(f32[1,256]{1,0:T(1,128)} %shard_map.77), kind=kLoop, calls=%fused_computation.1 | loop fusion | bytes 1024 | tf_op jit(solution)/shard_map/squeeze | solution.py:437

commit v2 on v1

--- a/solution.py
+++ b/solution.py
@@ -13,6 +13,7 @@
 RING = 4
 WSLOTS = 4
 WIDTH = 512
+HEAD = 128
 
 
 def largest_tile(columns, most):
@@ -23,10 +24,10 @@
 
 
 def kernel(dims, hidden, weight, targets, segment, mask, outside, out,
-           hx, hp, wbuf, ybuf, prt, qs, qr, ss, sr, scale_buf, tg, tcol, m_buf, s_buf, p_buf,
-           info, outv, denom, stat, statr, wsem, lsem, hsem, csem_s, csem_r, fsem_s, fsem_r,
-           tsem, isem, ysem, prsem, qssem, qrsem, sssem, srsem, stsem, dsem):
-    dp, nv, rows, depth, tiles, tile, chunks, rounds = dims
+           hx, hp, cx, wbuf, ybuf, prt, qs, qr, ss, sr, scale_buf, tg, tcol, m_buf, s_buf, p_buf,
+           info, outv, denom, stat, statr, wsem, wfirst, lsem, hsem, csem_s, csem_r, fsem_s, fsem_r,
+           tsem, isem, ysem, prsem, prfirst, qssem, qrsem, sssem, srsem, stsem, dsem):
+    dp, nv, rows, depth, tiles, tile, chunks, rounds, heads = dims
     chips = dp // 2
     me, v = lax.axis_index("dp"), lax.axis_index("vocab")
     x, c = me // 2, me % 2
@@ -35,6 +36,7 @@
     source = 2 * lax.rem(x + chips - 1, chips) + c
     share = rows // chunks
     total_steps = chips * tiles
+    extra = len(heads) - 1
 
     def remote(src, dst, send, recv, d, w):
         return pltpu.make_async_remote_copy(
@@ -54,51 +56,16 @@
     def chunk_rows(d, j):
         return pl.ds(pl.multiple_of(d * rows + j * share, share), share)
 
-    barrier = pltpu.get_barrier_semaphore()
-
-    def signal(sem, d, w):
-        pl.semaphore_signal(sem, inc=1, device_id=(d, w), device_id_type=pl.DeviceIdType.MESH)
-
-    for o in range(1, dp):
-        signal(barrier, lax.rem(me + o, dp), v)
-    pl.when(v >= 1)(lambda: signal(barrier, me, v - 1))
-    pl.when(v < nv - 1)(lambda: signal(barrier, me, v + 1))
-
-    to_stage = pltpu.make_async_copy(hidden.at[:, features(partner)], hp, lsem.at[0])
-    to_stage.start()
-    own = pltpu.make_async_copy(hidden.at[:, features(me)], hx.at[token_rows(me)], lsem.at[1])
-    own.start()
-    for k in range(min(WSLOTS - 1, total_steps)):
-        wcopy(k % tiles, k).start()
-
-    def sides(reach):
-        return jnp.where(v >= reach, 1, 0) + jnp.where(v < nv - reach, 1, 0)
-
-    pl.semaphore_wait(barrier, dp - 1 + sides(1))
-
-    def tell(k):
-        reach = 1 << k
-        pl.when(v >= reach)(lambda: signal(dsem.at[k], me, v - reach))
-        pl.when(v < nv - reach)(lambda: signal(dsem.at[k], me, v + reach))
-
-    def hear(k):
-        pl.semaphore_wait(dsem.at[k], sides(1 << k))
-
-    to_partner = remote(hp, hx.at[token_rows(me)], hsem.at[0], hsem.at[1], partner, v)
-    targets_copy = remote(targets, tg, tsem.at[0], tsem.at[1], source, v)
-
     def crossing(step, e):
         d = 2 * lax.rem(x + step, chips) + e
-        src = hidden.at[pl.ds(pl.multiple_of(v * share, share), share), features(d)]
-        i = 2 * (step - 1) + e
-        r = 2 * (chips - step - 1) + c
-        return d, src, i, r
+        return d, 2 * (step - 1) + e, 2 * (chips - step - 1) + c
 
     def cross_start():
+        pltpu.make_async_copy(cx, cx, lsem.at[4]).wait()
         for step in range(1, chips):
             for e in range(2):
-                d, src, i, r = crossing(step, e)
-                remote(src, hx.at[chunk_rows(me, v)], csem_s.at[i], csem_r.at[r], d, v).start()
+                d, i, r = crossing(step, e)
+                remote(cx.at[i], hx.at[chunk_rows(me, v)], csem_s.at[i], csem_r.at[r], d, v).start()
 
     def if_sender(fn):
         if chunks < nv:
@@ -106,11 +73,60 @@
         else:
             fn()
 
+    barrier = pltpu.get_barrier_semaphore()
+
+    def signal(sem, d, w):
+        pl.semaphore_signal(sem, inc=1, device_id=(d, w), device_id_type=pl.DeviceIdType.MESH)
+
+    for o in range(1, dp):
+        signal(barrier, lax.rem(me + o, dp), v)
+    pl.when(v >= 1)(lambda: signal(barrier, me, v - 1))
+    pl.when(v < nv - 1)(lambda: signal(barrier, me, v + 1))
+
+    to_stage = pltpu.make_async_copy(hidden.at[:, features(partner)], hp, lsem.at[0])
+    to_stage.start()
+
+    def cross_load():
+        for step in range(1, chips):
+            for e in range(2):
+                d, i, r = crossing(step, e)
+                src = hidden.at[pl.ds(pl.multiple_of(v * share, share), share), features(d)]
+                pltpu.make_async_copy(src, cx.at[i], lsem.at[4]).start()
+
+    if_sender(cross_load)
+    own = pltpu.make_async_copy(hidden.at[:, features(me)], hx.at[token_rows(me)], lsem.at[1])
+    own.start()
+
+    def first_copy(k):
+        cols = pl.ds(*heads[k])
+        return pltpu.make_async_copy(weight.at[:, cols], wbuf.at[0, :, cols], wfirst.at[k])
+
+    for k in range(len(heads)):
+        first_copy(k).start()
+
+    def sides(reach):
+        return jnp.where(v >= reach, 1, 0) + jnp.where(v < nv - reach, 1, 0)
+
+    pl.semaphore_wait(barrier, dp - 1 + sides(1))
+
+    def tell(k):
+        reach = 1 << k
+        pl.when(v >= reach)(lambda: signal(dsem.at[k], me, v - reach))
+        pl.when(v < nv - reach)(lambda: signal(dsem.at[k], me, v + reach))
+
+    def hear(k):
+        pl.semaphore_wait(dsem.at[k], sides(1 << k))
+
+    to_partner = remote(hp, hx.at[token_rows(me)], hsem.at[0], hsem.at[1], partner, v)
+    targets_copy = remote(targets, tg, tsem.at[0], tsem.at[1], source, v)
+
+    to_stage.wait()
+    to_partner.start()
     if_sender(cross_start)
     if rounds:
         tell(0)
-    to_stage.wait()
-    to_partner.start()
+    for k in range(1, min(WSLOTS, total_steps)):
+        wcopy(k % tiles, k).start()
 
     local_info = [pltpu.make_async_copy(ref, info.at[me, k], lsem.at[2])
                   for k, ref in enumerate((segment, mask))]
@@ -160,60 +176,67 @@
         else:
             blocks_wait(2 * (chunks - 1) * share, fsem_s.at[0], fsem_r.at[step - 1], False)
 
-    def dot_rows(start, count, at, slot, yslot):
+    def dot_rows(start, count, at, slot, yslot, first=0, width=tile):
         lhs = pl.ds(pl.multiple_of(start, count), count)
-        ybuf[yslot, pl.ds(pl.multiple_of(at, count), count), :] = jnp.dot(
-            hx[lhs, :], wbuf[slot], preferred_element_type=jnp.float32)
+        cols = slice(first, first + width)
+        ybuf[yslot, pl.ds(pl.multiple_of(at, count), count), cols] = jnp.dot(
+            hx[lhs, :], wbuf[slot, :, cols], preferred_element_type=jnp.float32)
 
     def ycopy(i):
         half = pl.ds(pl.multiple_of((1 - c) * rows, rows), rows)
         slot, ring = lax.rem(i, 2), lax.rem(i, RING)
         return remote(ybuf.at[slot, half], prt.at[ring], ysem.at[slot], prsem.at[ring], partner, v)
 
-    def qcopy(s, t):
+    def first_ycopy(k):
+        half = pl.ds(pl.multiple_of((1 - c) * rows, rows), rows)
+        cols = pl.ds(*heads[k])
+        return remote(ybuf.at[0, half, cols], prt.at[0, :, cols], ysem.at[0], prfirst.at[k], partner, v)
+
+    def qcopy(s, t, k, first, width):
         d = 2 * lax.rem(x + chips - s - 1 + chips, chips) + c
-        return (remote(qs.at[s, t], qr.at[s, t], qssem, qrsem.at[s, t], d, v),
-                remote(ss.at[s, t], sr.at[s, t], sssem, srsem.at[s, t], d, v))
+        cols = pl.ds(first, width)
+        return (remote(qs.at[s, t, :, cols], qr.at[s, t, :, cols], qssem, qrsem.at[s, k], d, v),
+                remote(ss.at[s, k], sr.at[s, k], sssem, srsem.at[s, k], d, v))
 
     band = min(rows, 32)
 
-    def total(i, b):
+    def total(i, b, cols):
         mine = pl.ds(pl.multiple_of(c * rows + b * band, band), band)
         theirs = pl.ds(b * band, band)
-        return ybuf[lax.rem(i, 2), mine, :] + prt[lax.rem(i, RING), theirs, :]
-
-    def send_sums(s, t):
+        return ybuf[lax.rem(i, 2), mine, cols] + prt[lax.rem(i, RING), theirs, cols]
+
+    def send_sums(s, t, k, first, width):
         i = s * tiles + t
-        ycopy(i).wait_recv()
+        cols = slice(first, first + width)
         for b in range(rows // band):
-            value = total(i, b)
+            value = total(i, b, cols)
             top = jnp.maximum(jnp.max(jnp.abs(value), axis=1, keepdims=True), TINY)
             code = jnp.round(value * (TOP / top)).astype(jnp.int32)
-            qs[s, t, b * band:(b + 1) * band, :] = code.astype(jnp.int16)
+            qs[s, t, b * band:(b + 1) * band, cols] = code.astype(jnp.int16)
             scale_buf[b * band:(b + 1) * band, :] = jnp.broadcast_to(top * (1.0 / TOP), (band, LANES))
-        data, scales = qcopy(s, t)
+        data, scales = qcopy(s, t, k, first, width)
         data.start()
-        ss[s, t] = jnp.transpose(scale_buf[0:rows, :])[0:1, :]
+        ss[s, k] = jnp.transpose(scale_buf[0:rows, :])[0:1, :]
         scales.start()
 
-    def finish(s, t):
+    def finish(s, t, k, first, width):
         i = s * tiles + t
-        ycopy(i).wait_recv()
         for a in range(chips - 1):
-            for copy in qcopy(a, t):
+            for copy in qcopy(a, t, k, first, width):
                 copy.wait_recv()
             scale_buf[a * rows:(a + 1) * rows, :] = jnp.transpose(
-                jnp.broadcast_to(sr[a, t], (LANES, rows)))
-        base = v * (tiles * tile) + t * tile
+                jnp.broadcast_to(sr[a, k], (LANES, rows)))
+        base = v * (tiles * tile) + t * tile + first
         lane = lax.broadcasted_iota(jnp.int32, (band, LANES), 1)
         for b in range(rows // band):
             here = slice(b * band, (b + 1) * band)
-            value = total(i, b)
+            value = total(i, b, slice(first, first + width))
             parts = []
-            for k in range(tile // LANES):
-                part = value[:, k * LANES:(k + 1) * LANES]
+            for j in range(width // LANES):
+                part = value[:, j * LANES:(j + 1) * LANES]
+                from_here = slice(first + j * LANES, first + (j + 1) * LANES)
                 for a in range(chips - 1):
-                    code = qr[a, t, here, k * LANES:(k + 1) * LANES].astype(jnp.int32)
+                    code = qr[a, t, here, from_here].astype(jnp.int32)
                     part = part + code.astype(jnp.float32) * scale_buf[a * rows + b * band:a * rows + (b + 1) * band, :]
                 parts.append(part)
             old = m_buf[here, :]
@@ -221,9 +244,9 @@
             acc = s_buf[here, :] * jnp.exp(old - new)
             picked = p_buf[here, :]
             wanted = tcol[here, :] - base
-            for k, part in enumerate(parts):
+            for j, part in enumerate(parts):
                 acc = acc + jnp.exp(part - new)
-                picked = picked + jnp.where(lane + k * LANES == wanted, part, 0.0)
+                picked = picked + jnp.where(lane + j * LANES == wanted, part, 0.0)
             m_buf[here, :] = new
             s_buf[here, :] = acc
             p_buf[here, :] = picked
@@ -269,7 +292,11 @@
             spread_wait(chips - s)
         if last:
             prepare()
-        handle = finish if last else send_sums
+        piece = finish if last else send_sums
+
+        def handle(t, s=s, piece=piece):
+            ycopy(s * tiles + t).wait_recv()
+            piece(s, t, t + extra, 0, tile)
 
         def begin(i):
             slot = lax.rem(i, WSLOTS)
@@ -292,28 +319,42 @@
             dot_rows(group * 2 * rows, 2 * rows, 0, slot, lax.rem(i, 2))
             ycopy(i).start()
 
-            @pl.when(t >= 1)
+            @pl.when(t >= 2)
             def _():
-                handle(s, t - 1)
+                handle(t - 1)
 
             if s == 0:
                 for at, event in events:
                     pl.when(t == min(at, tiles - 1))(event)
             return carry
 
-        first = 0
         if s == 0:
-            slot = begin(0)
-            dot_rows(me * rows, rows, c * rows, slot, 0)
+            for k in range(len(heads)):
+                first_copy(k).wait()
+                dot_rows(me * rows, rows, c * rows, 0, 0, *heads[k])
             to_partner.wait_recv()
-            dot_rows(partner * rows, rows, (1 - c) * rows, slot, 0)
-            ycopy(0).start()
-            for at, event in events:
-                if min(at, tiles - 1) == 0:
+            for k in range(len(heads)):
+                dot_rows(partner * rows, rows, (1 - c) * rows, 0, 0, *heads[k])
+                first_ycopy(k).start()
+            for k in range(len(heads)):
+                first_ycopy(k).wait_recv()
+                piece(s, 0, k, *heads[k])
+            if tiles == 1:
+                for at, event in events:
                     event()
-            first = 1
-        lax.fori_loop(first, tiles, step, 0)
-        handle(s, tiles - 1)
+        else:
+            i = s * tiles
+            slot = begin(i)
+            if i >= 2:
+                ycopy(i).wait_send()
+            dot_rows(group * 2 * rows, 2 * rows, 0, slot, i % 2)
+            ycopy(i).start()
+            ycopy(i).wait_recv()
+            for k in range(len(heads)):
+                piece(s, 0, k, *heads[k])
+        if tiles > 1:
+            lax.fori_loop(1, tiles, step, 0)
+            handle(tiles - 1)
 
     lane = lax.broadcasted_iota(jnp.int32, (rows, LANES), 1)
     peak = jnp.max(m_buf[...], axis=1, keepdims=True)
@@ -365,8 +406,8 @@
     def leave():
         for step in range(1, chips):
             for e in range(2):
-                d, src, i, r = crossing(step, e)
-                remote(src, hx.at[chunk_rows(me, v)], csem_s.at[i], csem_r.at[r], d, v).wait_send()
+                d, i, r = crossing(step, e)
+                remote(cx.at[i], hx.at[chunk_rows(me, v)], csem_s.at[i], csem_r.at[r], d, v).wait_send()
         for step in range(1, chips):
             for e in range(2):
                 i = 2 * (step - 1) + e
@@ -378,6 +419,12 @@
     remote(qs, qr, qssem, qrsem.at[0, 0], partner, v).wait_send()
     remote(ss, sr, sssem, srsem.at[0, 0], partner, v).wait_send()
     remote(most, most, stsem.at[0], stsem.at[1], partner, v).wait_send()
+
+
+def split(res, loss, sample):
+    rows, samples = loss.shape[1], sample.shape[1]
+    loss[...] = res[:, 0:rows]
+    sample[...] = res[:, rows:rows + samples]
 
 
 def solution(mesh):
@@ -391,8 +438,15 @@
         tile = largest_tile(columns, WIDTH)
         tiles = columns // tile
         chunks = min(nv, rows // 16)
+        share = rows // chunks
         rounds = (nv - 2).bit_length()
-        dims = (dp, nv, rows, depth, tiles, tile, chunks, rounds)
+        heads, at = [], 0
+        while at < tile:
+            width = HEAD if at < 2 * HEAD and tile > HEAD else tile - at
+            heads.append((at, width))
+            at += width
+        pieces = tiles + len(heads) - 1
+        dims = (dp, nv, rows, depth, tiles, tile, chunks, rounds, tuple(heads))
         sem = pltpu.SemaphoreType.DMA
         far = 2 * (chips - 1)
         wide = -(-samples // LANES) * LANES
@@ -400,19 +454,20 @@
         hbm = pl.BlockSpec(memory_space=pl.ANY)
         res = pl.pallas_call(
             functools.partial(kernel, dims),
-            out_shape=jax.ShapeDtypeStruct((1, rows + wide), jnp.float32),
+            out_shape=pltpu.VMEM((1, rows + wide), jnp.float32),
             in_specs=[hbm] * 6,
             out_specs=vm,
             scratch_shapes=[
                 pltpu.VMEM((dp * rows, depth), jnp.bfloat16),
                 pltpu.VMEM((rows, depth), jnp.bfloat16),
+                pltpu.VMEM((far, share, depth), jnp.bfloat16),
                 pltpu.VMEM((WSLOTS, depth, tile), jnp.bfloat16),
                 pltpu.VMEM((2, 2 * rows, tile), jnp.float32),
                 pltpu.VMEM((RING, rows, tile), jnp.float32),
                 pltpu.VMEM((chips - 1, tiles, rows, tile), jnp.int16),
                 pltpu.VMEM((chips - 1, tiles, rows, tile), jnp.int16),
-                pltpu.VMEM((chips - 1, tiles, 1, rows), jnp.float32),
-                pltpu.VMEM((chips - 1, tiles, 1, rows), jnp.float32),
+                pltpu.VMEM((chips - 1, pieces, 1, rows), jnp.float32),
+                pltpu.VMEM((chips - 1, pieces, 1, rows), jnp.float32),
                 pltpu.VMEM(((chips - 1) * rows, LANES), jnp.float32),
                 pltpu.VMEM((1, rows), jnp.int32),
                 pltpu.VMEM((rows, LANES), jnp.int32),
@@ -424,17 +479,25 @@
                 pltpu.VMEM((samples, LANES), jnp.float32),
                 pltpu.VMEM((2, rows), jnp.float32),
                 pltpu.VMEM((dp * nv, 2, rows), jnp.float32),
-                sem((WSLOTS,)), sem((4,)), sem((2,)), sem((far,)), sem((far,)),
+                sem((WSLOTS,)), sem((len(heads),)), sem((5,)), sem((2,)), sem((far,)), sem((far,)),
                 sem((far,)), sem((chips - 1,)), sem((2,)), sem((2,)),
-                sem((2,)), sem((RING,)),
-                sem, sem((chips - 1, tiles)), sem, sem((chips - 1, tiles)),
+                sem((2,)), sem((RING,)), sem((len(heads),)),
+                sem, sem((chips - 1, pieces)), sem, sem((chips - 1, pieces)),
                 sem((2,)), pltpu.SemaphoreType.REGULAR((max(rounds, 1),)),
             ],
             compiler_params=pltpu.CompilerParams(
-                collective_id=0, has_side_effects=True, vmem_limit_bytes=60 * 1024 * 1024),
+                collective_id=0, has_side_effects=True, vmem_limit_bytes=62 * 1024 * 1024),
         )(hidden, out_weight, targets[None, :], segment[None, :], loss_mask[None, :],
           outside_count[None, :])
-        return res[0, :rows], res[0, rows:rows + samples]
+        loss, sample = pl.pallas_call(
+            split,
+            out_shape=(jax.ShapeDtypeStruct((1, rows), jnp.float32),
+                       jax.ShapeDtypeStruct((1, samples), jnp.float32)),
+            in_specs=[vm],
+            out_specs=(vm, vm),
+            compiler_params=pltpu.CompilerParams(vmem_limit_bytes=1024 * 1024),
+        )(res)
+        return loss[0], sample[0]
 
     return jax.shard_map(
         body,

time: 87.9 us -> 85.5 us (0.973)
  local copies, waits for them, and re-layouts: 2.28 us -> 0 us
    squeeze x2 -> x0, local copies, waits for them, and re-layouts: 2.28 us -> none  [body(): return (res[0, :rows], res[0, rows:rows + samples])]
    pallas_call x1 -> x2, Pallas kernels: 84.8 us -> 84.7 us  [the longest x1 84.2 us: body(): pl.pallas_call(functools.partial(kernel, dims), out_shape=pltpu.VMEM((1,...]
where the time goes in v2:
time: 85.5 us; the launch traced here: 85.4 us
  Pallas kernels  84.7 us (99%)
    pallas_call x1, Pallas kernels, body(): pl.pallas_call(functools.partial(kernel, dims), out_shape=pltpu.VMEM((1,...  84.2 us

profile of v2, /device:TPU:0, one launch (start us, length us, event | category | flops | bytes accessed | tf_op | source)
XLA Modules:
  0.0 85.4 jit_solution(16844343540530529937)
XLA Ops:
  0.6 84.2 %shard_map.77.res = f32[1,256]{1,0:T(1,128)S(1)} custom-call(bf16[128,8192]{1,0:T(8,128)(2,1)} %hidden.1, bf16[2048,12288]{1,0:T(8,128)(2,1)} %weight.1, s32[1,128]{1,0:T(1,128)} %bitcast.6, s32[1,128]{1,0:T(1,128)} %bitcast.7, s32[1,128]{1,0:T(1,128)} %bitcast.8, s32[1,16]{1,0:T(1,128)} %bitcast.9), custom_call_target="tpu_custom_call" | custom-call | tf_op jit(solution)/shard_map/pallas_call | solution.py:455
  84.9 0.5 shard_map.78

commit v3 on v2

--- a/solution.py
+++ b/solution.py
@@ -27,7 +27,7 @@
            hx, hp, cx, wbuf, ybuf, prt, qs, qr, ss, sr, scale_buf, tg, tcol, m_buf, s_buf, p_buf,
            info, outv, denom, stat, statr, wsem, wfirst, lsem, hsem, csem_s, csem_r, fsem_s, fsem_r,
            tsem, isem, ysem, prsem, prfirst, qssem, qrsem, sssem, srsem, stsem, dsem):
-    dp, nv, rows, depth, tiles, tile, chunks, rounds, heads = dims
+    dp, nv, rows, depth, tiles, tile, chunks, rounds, heads, groups = dims
     chips = dp // 2
     me, v = lax.axis_index("dp"), lax.axis_index("vocab")
     x, c = me // 2, me % 2
@@ -58,14 +58,14 @@
 
     def crossing(step, e):
         d = 2 * lax.rem(x + step, chips) + e
-        return d, 2 * (step - 1) + e, 2 * (chips - step - 1) + c
+        return d, 2 * (step - 1) + e, chips - step - 1
 
     def cross_start():
         pltpu.make_async_copy(cx, cx, lsem.at[4]).wait()
         for step in range(1, chips):
             for e in range(2):
                 d, i, r = crossing(step, e)
-                remote(cx.at[i], hx.at[chunk_rows(me, v)], csem_s.at[i], csem_r.at[r], d, v).start()
+                remote(cx.at[i], hx.at[chunk_rows(me, v)], csem_s, csem_r.at[r], d, v).start()
 
     def if_sender(fn):
         if chunks < nv:
@@ -146,11 +146,11 @@
 
     def spread():
         for step in range(1, chips):
+            blocks_wait(2 * share, csem_s, csem_r.at[step - 1], False)
             for e in range(2):
                 d = 2 * lax.rem(x + step, chips) + e
                 i = 2 * (step - 1) + e
                 block = hx.at[chunk_rows(d, v)]
-                remote(block, block, csem_s.at[i], csem_r.at[i], d, v).wait_recv()
 
                 def one(o, carry, block=block, step=step, i=i):
                     w = lax.rem(v + o, nv)
@@ -195,8 +195,17 @@
     def qcopy(s, t, k, first, width):
         d = 2 * lax.rem(x + chips - s - 1 + chips, chips) + c
         cols = pl.ds(first, width)
-        return (remote(qs.at[s, t, :, cols], qr.at[s, t, :, cols], qssem, qrsem.at[s, k], d, v),
-                remote(ss.at[s, k], sr.at[s, k], sssem, srsem.at[s, k], d, v))
+        g = sum(jnp.where(t >= start, 1, 0) for start, _ in groups[1:]) if len(groups) > 1 else 0
+        return (remote(qs.at[s, t, :, cols], qr.at[s, t, :, cols], qssem, qrsem.at[s, g], d, v),
+                remote(ss.at[s, k], sr.at[s, k], sssem, srsem.at[s, g], d, v))
+
+    def group_wait(g):
+        start, count = groups[g]
+        low, high = (start + extra if start else 0), start + count + extra
+        for a in range(chips - 1):
+            block, scales = qr.at[a, pl.ds(start, count)], sr.at[a, pl.ds(low, high - low)]
+            remote(block, block, qssem, qrsem.at[a, g], partner, v).wait_recv()
+            remote(scales, scales, sssem, srsem.at[a, g], partner, v).wait_recv()
 
     band = min(rows, 32)
 
@@ -222,8 +231,6 @@
     def finish(s, t, k, first, width):
         i = s * tiles + t
         for a in range(chips - 1):
-            for copy in qcopy(a, t, k, first, width):
-                copy.wait_recv()
             scale_buf[a * rows:(a + 1) * rows, :] = jnp.transpose(
                 jnp.broadcast_to(sr[a, k], (LANES, rows)))
         base = v * (tiles * tile) + t * tile + first
@@ -294,8 +301,12 @@
             prepare()
         piece = finish if last else send_sums
 
-        def handle(t, s=s, piece=piece):
+        def handle(t, s=s, piece=piece, last=last):
             ycopy(s * tiles + t).wait_recv()
+            if last:
+                for g, (start, _) in enumerate(groups):
+                    if start > 0:
+                        pl.when(t == start)(functools.partial(group_wait, g))
             piece(s, t, t + extra, 0, tile)
 
         def begin(i):
@@ -336,6 +347,8 @@
             for k in range(len(heads)):
                 dot_rows(partner * rows, rows, (1 - c) * rows, 0, 0, *heads[k])
                 first_ycopy(k).start()
+            if last:
+                group_wait(0)
             for k in range(len(heads)):
                 first_ycopy(k).wait_recv()
                 piece(s, 0, k, *heads[k])
@@ -350,6 +363,8 @@
             dot_rows(group * 2 * rows, 2 * rows, 0, slot, i % 2)
             ycopy(i).start()
             ycopy(i).wait_recv()
+            if last:
+                group_wait(0)
             for k in range(len(heads)):
                 piece(s, 0, k, *heads[k])
         if tiles > 1:
@@ -404,10 +419,7 @@
     remote(most_info, most_info, isem.at[0], isem.at[1], partner, v).wait_send()
 
     def leave():
-        for step in range(1, chips):
-            for e in range(2):
-                d, i, r = crossing(step, e)
-                remote(cx.at[i], hx.at[chunk_rows(me, v)], csem_s.at[i], csem_r.at[r], d, v).wait_send()
+        remote(cx, cx, csem_s, csem_r.at[0], partner, v).wait_send()
         for step in range(1, chips):
             for e in range(2):
                 i = 2 * (step - 1) + e
@@ -446,7 +458,13 @@
             heads.append((at, width))
             at += width
         pieces = tiles + len(heads) - 1
-        dims = (dp, nv, rows, depth, tiles, tile, chunks, rounds, tuple(heads))
+        groups, left, count = [], tiles, 1
+        while left:
+            count = min(count, left) if left > 2 * count or left <= count else left
+            groups.append((left - count, count))
+            left, count = left - count, count + 1
+        groups.reverse()
+        dims = (dp, nv, rows, depth, tiles, tile, chunks, rounds, tuple(heads), tuple(groups))
         sem = pltpu.SemaphoreType.DMA
         far = 2 * (chips - 1)
         wide = -(-samples // LANES) * LANES
@@ -479,10 +497,10 @@
                 pltpu.VMEM((samples, LANES), jnp.float32),
                 pltpu.VMEM((2, rows), jnp.float32),
                 pltpu.VMEM((dp * nv, 2, rows), jnp.float32),
-                sem((WSLOTS,)), sem((len(heads),)), sem((5,)), sem((2,)), sem((far,)), sem((far,)),
+                sem((WSLOTS,)), sem((len(heads),)), sem((5,)), sem((2,)), sem, sem((chips - 1,)),
                 sem((far,)), sem((chips - 1,)), sem((2,)), sem((2,)),
                 sem((2,)), sem((RING,)), sem((len(heads),)),
-                sem, sem((chips - 1, pieces)), sem, sem((chips - 1, pieces)),
+                sem, sem((chips - 1, len(groups))), sem, sem((chips - 1, len(groups))),
                 sem((2,)), pltpu.SemaphoreType.REGULAR((max(rounds, 1),)),
             ],
             compiler_params=pltpu.CompilerParams(

time: 85.5 us -> 85.2 us (level)
  no operation moved by 1% of the time
where the time goes in v3:
time: 85.2 us; the launch traced here: 85 us
  Pallas kernels  84.4 us (99%)
    pallas_call x1, Pallas kernels, body(): pl.pallas_call(functools.partial(kernel, dims), out_shape=pltpu.VMEM((1,...  83.8 us

profile of v3, /device:TPU:0, one launch (start us, length us, event | category | flops | bytes accessed | tf_op | source)
XLA Modules:
  0.0 85.0 jit_solution(12696339736297419158)
XLA Ops:
  0.6 83.8 %shard_map.77.res = f32[1,256]{1,0:T(1,128)S(1)} custom-call(bf16[128,8192]{1,0:T(8,128)(2,1)} %hidden.1, bf16[2048,12288]{1,0:T(8,128)(2,1)} %weight.1, s32[1,128]{1,0:T(1,128)} %bitcast.6, s32[1,128]{1,0:T(1,128)} %bitcast.7, s32[1,128]{1,0:T(1,128)} %bitcast.8, s32[1,16]{1,0:T(1,128)} %bitcast.9), custom_call_target="tpu_custom_call" | custom-call | tf_op jit(solution)/shard_map/pallas_call | solution.py:473
  84.5 0.5 shard_map.78

commit v4 on v3

--- a/solution.py
+++ b/solution.py
@@ -84,7 +84,6 @@
     pl.when(v < nv - 1)(lambda: signal(barrier, me, v + 1))
 
     to_stage = pltpu.make_async_copy(hidden.at[:, features(partner)], hp, lsem.at[0])
-    to_stage.start()
 
     def cross_load():
         for step in range(1, chips):
@@ -94,6 +93,7 @@
                 pltpu.make_async_copy(src, cx.at[i], lsem.at[4]).start()
 
     if_sender(cross_load)
+    to_stage.start()
     own = pltpu.make_async_copy(hidden.at[:, features(me)], hx.at[token_rows(me)], lsem.at[1])
     own.start()
 
@@ -120,9 +120,9 @@
     to_partner = remote(hp, hx.at[token_rows(me)], hsem.at[0], hsem.at[1], partner, v)
     targets_copy = remote(targets, tg, tsem.at[0], tsem.at[1], source, v)
 
+    if_sender(cross_start)
     to_stage.wait()
     to_partner.start()
-    if_sender(cross_start)
     if rounds:
         tell(0)
     for k in range(1, min(WSLOTS, total_steps)):
@@ -347,13 +347,20 @@
             for k in range(len(heads)):
                 dot_rows(partner * rows, rows, (1 - c) * rows, 0, 0, *heads[k])
                 first_ycopy(k).start()
+            ahead = tiles > 1 and not last
+            if ahead:
+                slot = begin(1)
+                dot_rows(partner * rows, rows, (1 - c) * rows, slot, 1)
+                ycopy(1).start()
             if last:
                 group_wait(0)
             for k in range(len(heads)):
                 first_ycopy(k).wait_recv()
                 piece(s, 0, k, *heads[k])
-            if tiles == 1:
-                for at, event in events:
+            if ahead:
+                dot_rows(me * rows, rows, c * rows, slot, 1)
+            for at, event in events:
+                if min(at, tiles - 1) <= int(ahead):
                     event()
         else:
             i = s * tiles
@@ -368,7 +375,7 @@
             for k in range(len(heads)):
                 piece(s, 0, k, *heads[k])
         if tiles > 1:
-            lax.fori_loop(1, tiles, step, 0)
+            lax.fori_loop(2 if s == 0 and ahead else 1, tiles, step, 0)
             handle(tiles - 1)
 
     lane = lax.broadcasted_iota(jnp.int32, (rows, LANES), 1)

time: 85.2 us -> 85.2 us (level)
  no operation moved by 1% of the time
where the time goes in v4:
time: 85.2 us; the launch traced here: 85.1 us
  Pallas kernels  84.4 us (99%)
    pallas_call x1, Pallas kernels, body(): pl.pallas_call(functools.partial(kernel, dims), out_shape=pltpu.VMEM((1,...  83.9 us

profile of v4, /device:TPU:0, one launch (start us, length us, event | category | flops | bytes accessed | tf_op | source)
XLA Modules:
  0.0 85.1 jit_solution(14820779468007905465)
XLA Ops:
  0.6 83.9 %shard_map.77.res = f32[1,256]{1,0:T(1,128)S(1)} custom-call(bf16[128,8192]{1,0:T(8,128)(2,1)} %hidden.1, bf16[2048,12288]{1,0:T(8,128)(2,1)} %weight.1, s32[1,128]{1,0:T(1,128)} %bitcast.6, s32[1,128]{1,0:T(1,128)} %bitcast.7, s32[1,128]{1,0:T(1,128)} %bitcast.8, s32[1,16]{1,0:T(1,128)} %bitcast.9), custom_call_target="tpu_custom_call" | custom-call | tf_op jit(solution)/shard_map/pallas_call | solution.py:480
  84.6 0.5 shard_map.78
